TPU v7x, 32 devices: a whole 2x2x4 slice. The times are simulated.
32 devices in a mesh: layer: 4 (over y, core), slab: 8 (over z, x).
Axes of the slice: x: 2, y: 2, z: 4, core: 2. Of those that a mesh axis runs over, the one named last changes fastest.
Arguments:
- weights: bfloat16 [8192, 16384], P('slab', 'layer'), may hold values from -0.29882812 to 0.29882812
- whitening: bfloat16 [8192, 8192], P('slab'), may hold values from -1 to 10, as said below
- test_matrix: int32 [16384, 1024], P(('layer', 'slab')), may hold values from -4 to 4
Outputs:
- basis: float32 [8192, 1024], P('slab')
- coefficients: float32 [16384, 1024], P('layer', 'slab')
Inputs may be any that keep to these rules, and one draw needn't show every extreme that they name: whitening is lower triangular with diagonal entries between 1 and 10.
All inputs are finite; a program needn't handle non-finite values.
Results may differ from a plain program's by a relative error of at most 0.006.
Values may be sent and summed in bfloat16 or wider, within the bound.
A program may use at most 128 MiB of HBM per device.

v0:
```python
import math
import jax
import jax.numpy as jnp
from jax import lax
from jax.sharding import PartitionSpec as P

D = 8192


def on_device(weights, whitening, test_matrix):
    rank_width = test_matrix.shape[1]
    slice_width = rank_width // lax.axis_size("layer")
    test_values = test_matrix.astype(jnp.bfloat16)
    columns = weights
    sketch_terms = jnp.dot(
        columns,
        lax.all_gather(test_values, "slab", axis=0, tiled=True),
        preferred_element_type=jnp.float32,
    )
    sketch = lax.psum_scatter(sketch_terms, "layer", scatter_dimension=1, tiled=True).astype(
        jnp.bfloat16
    )
    columns = whitening
    whitened_part = jnp.dot(
        columns,
        lax.all_gather(sketch, "slab", axis=0, tiled=True),
        preferred_element_type=jnp.float32,
    )
    whitened = lax.all_gather(whitened_part, "layer", axis=1, tiled=True)
    local_gram = jnp.dot(
        whitened.T, whitened, precision=lax.Precision.HIGHEST, preferred_element_type=jnp.float32
    )
    gram_matrix = lax.psum(local_gram, "slab")
    factor = jnp.linalg.cholesky(gram_matrix)
    ortho = jax.scipy.linalg.solve_triangular(factor, whitened.T, lower=True).T
    basis_half = ortho.astype(jnp.bfloat16)
    basis = basis_half.astype(jnp.float32) * math.sqrt(D)
    own_slice = lax.dynamic_slice_in_dim(
        basis_half, lax.axis_index("layer") * slice_width, slice_width, 1
    )
    columns = whitening
    projected_part = lax.psum_scatter(
        lax.dot_general(
            columns, own_slice, (((0,), (0,)), ((), ())), preferred_element_type=jnp.float32
        ),
        "slab",
        scatter_dimension=0,
        tiled=True,
    ).astype(jnp.bfloat16)
    projected = lax.all_gather(projected_part, "layer", axis=1, tiled=True)
    columns = weights
    coefficients = lax.psum_scatter(
        lax.dot_general(
            columns, projected, (((0,), (0,)), ((), ())), preferred_element_type=jnp.float32
        ),
        "slab",
        scatter_dimension=1,
        tiled=True,
    )
    return (basis, coefficients)


def solution(mesh):
    placed = (P("slab", "layer"), P("slab", None), P(("layer", "slab"), None))
    return jax.shard_map(
        on_device,
        mesh=mesh,
        in_specs=placed,
        out_specs=(P("slab", None), P("layer", "slab")),
        check_vma=False,
    )
```

profile of v0, /device:TPU:0, one launch (start us, length us, event | category | flops | bytes accessed | tf_op | source)
XLA Modules:
  0.0 1321.0 jit_solution(4433787939744664165)
XLA Ops:
  10.1 127.8 %all-gather.5.cloned.1.call-done = bf16[4096,1024]{1,0:T(8,128)(2,1)} async-done(((bf16[512,1024]{1,0:T(8,128)(2,1)}), bf16[4096,1024]{1,0:T(8,128)(2,1)}) %all-gather.5.cloned.1.call-update) | async-done | bytes 8388624 | tf_op jit(solution)/shard_map/all_gather | solution.py:17
  137.9 14.9 %fusion.73 = f32[1024,1024]{1,0:T(8,128)} fusion(bf16[1024,4096]{1,0:T(8,128)(2,1)} %param.3, bf16[4096,1024]{1,0:T(8,128)(2,1)} %all-gather.5.cloned.1.call-done), kind=kOutput, calls=%fused_computation.164 | convolution fusion | flops 8589934592 | bytes 20971520 | tf_op jit(solution)/shard_map/dot_general | solution.py:15
  152.9 42.7 %reduce-scatter.4.cloned.1.call-done = f32[1024,256]{1,0:T(8,128)} async-done(((f32[1024,1024]{1,0:T(8,128)}), f32[1024,256]{1,0:T(8,128)}) %reduce-scatter.4.cloned.1.call-update) | async-done | bytes 1048592 | tf_op jit(solution)/shard_map/reduce_scatter | solution.py:20
  197.8 73.4 %all-gather.7.cloned.1.call-done = bf16[8192,256]{1,0:T(8,128)(2,1)} async-done(((bf16[1024,256]{1,0:T(8,128)(2,1)}), bf16[8192,256]{1,0:T(8,128)(2,1)}) %all-gather.7.cloned.1.call-update) | async-done | bytes 4194320 | tf_op jit(solution)/shard_map/all_gather | solution.py:26
  271.1 12.6 convolution_bitcast_fusion.2
  284.0 32.9 %all-gather.9.cloned.1.call-done = f32[1024,1024]{0,1:T(8,128)} async-done(((f32[1024,256]{0,1:T(8,128)}), f32[1024,1024]{0,1:T(8,128)}) %all-gather.9.cloned.1.call-update) | async-done | bytes 4194320 | tf_op jit(solution)/shard_map/all_gather | solution.py:29
  316.9 18.2 %fusion.74 = f32[1024,1024]{0,1:T(8,128)} fusion(f32[1024,1024]{0,1:T(8,128)} %all-gather.9.cloned.1.call-done), kind=kOutput, calls=%fused_computation.165 | convolution fusion | flops 12884901888 | bytes 8388608 | tf_op jit(solution)/shard_map/dot_general | solution.py:30
  335.2 156.5 %all-reduce.3.cloned.1.call-done = f32[1024,1024]{0,1:T(8,128)} async-done(((f32[1024,1024]{0,1:T(8,128)}), f32[1024,1024]{0,1:T(8,128)}) %all-reduce.3.cloned.1.call-update) | async-done | bytes 4194320 | tf_op jit(solution)/shard_map/psum | solution.py:33
  503.8 11.7 cholesky.223
  515.5 9.8 custom-call.63
  531.8 11.9 cholesky.244
  557.4 11.7 cholesky.468
  583.7 11.9 cholesky.487
  610.1 11.7 cholesky.506
  623.1 10.2 custom-call.67
  636.6 11.7 cholesky.526
  662.4 11.9 cholesky.546
  688.0 11.7 cholesky.564
  711.4 22.8 %while.1 = (s32[]{:T(128)}, f32[1024,1024]{1,0:T(8,128)}, s32[8,2]{0,1:T(2,128)S(1)}, f32[8,128,128]{2,1,0:T(8,128)S(1)}, s32[]{:T(128)}) while((s32[]{:T(128)}, f32[1024,1024]{1,0:T(8,128)}, s32[8,2]{0,1:T(2,128)S(1)}, f32[8,128,128]{2,1,0:T(8,128)S(1)}, s32[]{:T(128)}) %tuple.58), condition=%wide.while_cond, body=%wide.while_body.sunk | while | flops 2 | bytes 131181 | solution.py:35
  734.2 78.8 %custom-call.70 = f32[8,128,128]{1,2,0:T(8,128)S(1)} custom-call(f32[8,128,128]{2,1,0:T(8,128)S(1)} %get-tuple-element.9), custom_call_target="InvertDiagBlocksLowerTriangular" | custom-call | tf_op jit(solution)/shard_map/jit(_solve_triangular)/triangular_solve | solution.py:35
  844.3 147.0 %reduce-scatter.6.cloned.1.call-done = f32[1024,256]{0,1:T(8,128)} async-done(((f32[8192,256]{0,1:T(8,128)}), f32[1024,256]{0,1:T(8,128)}) %reduce-scatter.6.cloned.1.call-update) | async-done | bytes 1048592 | tf_op jit(solution)/shard_map/reduce_scatter | solution.py:42
  993.5 21.8 %all-gather.11.cloned.1.call-done = bf16[1024,1024]{0,1:T(8,128)(2,1)} async-done(((bf16[1024,256]{0,1:T(8,128)(2,1)}), bf16[1024,1024]{0,1:T(8,128)(2,1)}) %all-gather.11.cloned.1.call-update) | async-done | bytes 2097168 | tf_op jit(solution)/shard_map/all_gather | solution.py:50
  1015.2 16.0 %convolution_bitcast_fusion.1 = f32[4096,1024]{0,1:T(8,128)} fusion(bf16[1024,1024]{0,1:T(8,128)(2,1)} %all-gather.11.cloned.1.call-done, bf16[1024,4096]{1,0:T(8,128)(2,1)} %param.3), kind=kOutput, calls=%fused_computation.3 | convolution fusion | flops 8589934592 | bytes 27262976 | tf_op jit(solution)/shard_map/dot_general | solution.py:53
  1039.1 271.7 %reduce-scatter.8.cloned.1.call-done = f32[4096,128]{0,1:T(8,128)} async-done(((f32[4096,1024]{0,1:T(8,128)}), f32[4096,128]{0,1:T(8,128)}) %reduce-scatter.8.cloned.1.call-update) | async-done | bytes 2097168 | tf_op jit(solution)/shard_map/reduce_scatter | solution.py:52
  (130 shorter events, 172.6 us)
Async XLA Ops:
  7.2 130.7 %all-gather.5.cloned.1.call-start = ((), (), s32[]{:S(2)}) async-start(), calls=%async_computation.3 | async-start | bytes 9437184 | tf_op jit(solution)/shard_map/all_gather | solution.py:17
  10.0 185.6 %reduce-scatter.4.cloned.1.call-start = ((), (), s32[]{:S(2)}) async-start(), calls=%async_computation.4 | async-start | bytes 5242880 | tf_op jit(solution)/shard_map/reduce_scatter | solution.py:20
  152.9 118.3 %all-gather.7.cloned.1.call-start = ((), (), s32[]{:S(2)}) async-start(), calls=%async_computation.5 | async-start | bytes 4718592 | tf_op jit(solution)/shard_map/all_gather | solution.py:26
  197.7 119.2 %all-gather.9.cloned.1.call-start = ((), (), s32[]{:S(2)}) async-start(), calls=%async_computation.6 | async-start | bytes 5242880 | tf_op jit(solution)/shard_map/all_gather | solution.py:29
  283.7 207.9 %all-reduce.3.cloned.1.call-start = ((), (), s32[]{:S(2)}) async-start(), calls=%async_computation.7 | async-start | bytes 8388608 | tf_op jit(solution)/shard_map/psum | solution.py:33
  335.1 656.2 %reduce-scatter.6.cloned.1.call-start = ((), (), s32[]{:S(2)}) async-start(), calls=%async_computation.8 | async-start | bytes 9437184 | tf_op jit(solution)/shard_map/reduce_scatter | solution.py:42
  501.8 2.0 copy-start
  813.1 4.3 copy-start.1
  822.3 15.2 %slice-start = ((s8[16777216]{0:T(1024)(128)(4,1)}), s8[4194304]{0:T(1024)(128)(4,1)S(1)}, s32[]{:S(2)}) async-start(s8[16777216]{0:T(1024)(128)(4,1)} %bitcast.119), calls=%async_computation.11 | async-start | bytes 8388608
  825.5 12.0 slice-start.1
  826.0 11.6 slice-start.2
  829.7 7.9 slice-start.3
  844.3 171.0 %all-gather.11.cloned.1.call-start = ((), (), s32[]{:S(2)}) async-start(), calls=%async_computation.9 | async-start | bytes 2621440 | tf_op jit(solution)/shard_map/all_gather | solution.py:50
  993.4 317.4 %reduce-scatter.8.cloned.1.call-start = ((), (), s32[]{:S(2)}) async-start(), calls=%async_computation.10 | async-start | bytes 18874368 | tf_op jit(solution)/shard_map/reduce_scatter | solution.py:52
Sparse Core Ops, SparseCore 0:
  10.7 127.1 all-gather.4
  153.0 42.5 reduce-scatter.3
  198.3 72.7 all-gather.6
  283.9 32.9 all-gather.8
  335.2 156.3 all-reduce.2
  844.4 146.8 reduce-scatter.5
  993.5 21.6 all-gather.10
  1031.3 279.4 reduce-scatter.7
where the time goes:
time: 1330 us; the launch traced here: 1320 us
  waiting for transfers between devices  874 us (66%)
  other arithmetic  270 us (20%)
  matrix products  115 us (9%)
  local copies, waits for them, and re-layouts  42.1 us (3%)
  between operations  19.9 us (1%)
    reduce_scatter x1, waiting for transfers between devices, on_device(): lax.psum_scatter(lax.dot_general(columns, projected, (((0,), (0,)), ((),...  272 us
    another operation x30, other arithmetic, on_device(): factor = jnp.linalg.cholesky(gram_matrix)  172 us
    psum x1, waiting for transfers between devices, on_device(): gram_matrix = lax.psum(local_gram, 'slab')  156 us
    reduce_scatter x1, waiting for transfers between devices, on_device(): lax.psum_scatter(lax.dot_general(columns, own_slice, (((0,), (0,)), ((),...  147 us
    all_gather x1, waiting for transfers between devices, on_device(): lax.all_gather(test_values, 'slab', axis=0, tiled=True)  128 us
    another operation x3, other arithmetic, on_device(): ortho = jax.scipy.linalg.solve_triangular(factor, whitened.T, lower=True).T  83.7 us
    all_gather x1, waiting for transfers between devices, on_device(): lax.all_gather(sketch, 'slab', axis=0, tiled=True)  73.4 us
    reduce_scatter x1, waiting for transfers between devices, on_device(): lax.psum_scatter(sketch_terms, 'layer', scatter_dimension=1, tiled=True)  42.7 us
  transfers between devices with their start and end apart: 8, of which 8 were waited for; matrix products, arithmetic and copies ran while one was open for 1% of the time, Pallas kernels for 0%

commit v1 on v0

--- a/solution.py
+++ b/solution.py
@@ -23,7 +23,9 @@
     columns = whitening
     whitened_part = jnp.dot(
         columns,
-        lax.all_gather(sketch, "slab", axis=0, tiled=True),
+        jnp.concatenate(
+            lax.all_to_all(jnp.stack([sketch] * lax.axis_size("slab")), "slab", 0, 0), axis=0
+        ),
         preferred_element_type=jnp.float32,
     )
     whitened = lax.all_gather(whitened_part, "layer", axis=1, tiled=True)

time: 1330 us -> 1350 us (1.015)
  blocking collectives: 0 us -> 98.4 us
  waiting for transfers between devices: 874 us -> 800 us
    all_to_all x0 -> x1, blocking collectives: none -> 98.4 us  [on_device(): lax.all_to_all(jnp.stack([sketch] * lax.axis_size('slab')), 'slab', 0, 0)]
    all_gather x1 -> x0, waiting for transfers between devices: 73.4 us -> none  [on_device(): lax.all_gather(sketch, 'slab', axis=0, tiled=True)]
  transfers between devices with their start and end apart: 8 -> 7, of which waited for: 8 -> 7; matrix products, arithmetic and copies ran while one was open for 1% -> 1% of each run, Pallas kernels for 0% -> 0%
where the time goes in v1:
time: 1350 us; the launch traced here: 1340 us
  waiting for transfers between devices  800 us (59%)
  other arithmetic  269 us (20%)
  matrix products  115 us (9%)
  blocking collectives  98.4 us (7%)
  local copies, waits for them, and re-layouts  42.4 us (3%)
  between operations  19.9 us (1%)
    reduce_scatter x1, waiting for transfers between devices, on_device(): lax.psum_scatter(lax.dot_general(columns, projected, (((0,), (0,)), ((),...  272 us
    another operation x30, other arithmetic, on_device(): factor = jnp.linalg.cholesky(gram_matrix)  172 us
    psum x1, waiting for transfers between devices, on_device(): gram_matrix = lax.psum(local_gram, 'slab')  156 us
    reduce_scatter x1, waiting for transfers between devices, on_device(): lax.psum_scatter(lax.dot_general(columns, own_slice, (((0,), (0,)), ((),...  147 us
    all_gather x1, waiting for transfers between devices, on_device(): lax.all_gather(test_values, 'slab', axis=0, tiled=True)  128 us
    all_to_all x1, blocking collectives, on_device(): lax.all_to_all(jnp.stack([sketch] * lax.axis_size('slab')), 'slab', 0, 0)  98.4 us
    another operation x3, other arithmetic, on_device(): ortho = jax.scipy.linalg.solve_triangular(factor, whitened.T, lower=True).T  83.7 us
    reduce_scatter x1, waiting for transfers between devices, on_device(): lax.psum_scatter(sketch_terms, 'layer', scatter_dimension=1, tiled=True)  42.7 us
  transfers between devices with their start and end apart: 7, of which 7 were waited for; matrix products, arithmetic and copies ran while one was open for 1% of the time, Pallas kernels for 0%

profile of v1, /device:TPU:0, one launch (start us, length us, event | category | flops | bytes accessed | tf_op | source)
XLA Modules:
  0.0 1345.0 jit_solution(10391996027569151313)
XLA Ops:
  10.1 127.8 %all-gather.4.cloned.1.call-done = bf16[4096,1024]{1,0:T(8,128)(2,1)} async-done(((bf16[512,1024]{1,0:T(8,128)(2,1)}), bf16[4096,1024]{1,0:T(8,128)(2,1)}) %all-gather.4.cloned.1.call-update) | async-done | bytes 8388624 | tf_op jit(solution)/shard_map/all_gather | solution.py:17
  137.9 14.9 %fusion.73 = f32[1024,1024]{1,0:T(8,128)} fusion(bf16[1024,4096]{1,0:T(8,128)(2,1)} %param.3, bf16[4096,1024]{1,0:T(8,128)(2,1)} %all-gather.4.cloned.1.call-done), kind=kOutput, calls=%fused_computation.164 | convolution fusion | flops 8589934592 | bytes 20971520 | tf_op jit(solution)/shard_map/dot_general | solution.py:15
  152.9 42.7 %reduce-scatter.4.cloned.1.call-done = f32[1024,256]{1,0:T(8,128)} async-done(((f32[1024,1024]{1,0:T(8,128)}), f32[1024,256]{1,0:T(8,128)}) %reduce-scatter.4.cloned.1.call-update) | async-done | bytes 1048592 | tf_op jit(solution)/shard_map/reduce_scatter | solution.py:20
  197.2 98.4 %all_to_all.5 = bf16[8,1024,256]{2,1,0:T(8,128)(2,1)} all-to-all(bf16[8,1024,256]{2,1,0:T(8,128)(2,1)S(1)} %stack.2), channel_id=1, replica_groups=mesh['layer'=4,'slab'=8] {'slab'}, dimensions={0} | all-to-all | bytes 8388608 | tf_op jit(solution)/shard_map/all_to_all | solution.py:27
  295.6 12.6 convolution_bitcast_fusion.2
  308.5 32.4 %all-gather.6.cloned.1.call-done = f32[1024,1024]{0,1:T(8,128)} async-done(((f32[1024,256]{0,1:T(8,128)}), f32[1024,1024]{0,1:T(8,128)}) %all-gather.6.cloned.1.call-update) | async-done | bytes 4194320 | tf_op jit(solution)/shard_map/all_gather | solution.py:31
  340.9 18.2 %fusion.74 = f32[1024,1024]{0,1:T(8,128)} fusion(f32[1024,1024]{0,1:T(8,128)} %all-gather.6.cloned.1.call-done), kind=kOutput, calls=%fused_computation.165 | convolution fusion | flops 12884901888 | bytes 8388608 | tf_op jit(solution)/shard_map/dot_general | solution.py:32
  359.2 156.5 %all-reduce.3.cloned.1.call-done = f32[1024,1024]{0,1:T(8,128)} async-done(((f32[1024,1024]{0,1:T(8,128)}), f32[1024,1024]{0,1:T(8,128)}) %all-reduce.3.cloned.1.call-update) | async-done | bytes 4194320 | tf_op jit(solution)/shard_map/psum | solution.py:35
  527.8 11.7 cholesky.223
  539.5 9.8 custom-call.63
  555.8 11.9 cholesky.244
  581.4 11.7 cholesky.468
  607.7 11.9 cholesky.487
  634.1 11.7 cholesky.506
  647.1 10.2 custom-call.67
  660.6 11.7 cholesky.526
  686.4 11.9 cholesky.546
  711.9 11.7 cholesky.564
  735.4 22.8 %while.1 = (s32[]{:T(128)}, f32[1024,1024]{1,0:T(8,128)}, s32[8,2]{0,1:T(2,128)S(1)}, f32[8,128,128]{2,1,0:T(8,128)S(1)}, s32[]{:T(128)}) while((s32[]{:T(128)}, f32[1024,1024]{1,0:T(8,128)}, s32[8,2]{0,1:T(2,128)S(1)}, f32[8,128,128]{2,1,0:T(8,128)S(1)}, s32[]{:T(128)}) %tuple.58), condition=%wide.while_cond, body=%wide.while_body.sunk | while | flops 2 | bytes 131181 | solution.py:37
  758.2 78.8 %custom-call.70 = f32[8,128,128]{1,2,0:T(8,128)S(1)} custom-call(f32[8,128,128]{2,1,0:T(8,128)S(1)} %get-tuple-element.9), custom_call_target="InvertDiagBlocksLowerTriangular" | custom-call | tf_op jit(solution)/shard_map/jit(_solve_triangular)/triangular_solve | solution.py:37
  868.3 147.0 %reduce-scatter.6.cloned.1.call-done = f32[1024,256]{0,1:T(8,128)} async-done(((f32[8192,256]{0,1:T(8,128)}), f32[1024,256]{0,1:T(8,128)}) %reduce-scatter.6.cloned.1.call-update) | async-done | bytes 1048592 | tf_op jit(solution)/shard_map/reduce_scatter | solution.py:44
  1017.4 21.8 %all-gather.8.cloned.1.call-done = bf16[1024,1024]{0,1:T(8,128)(2,1)} async-done(((bf16[1024,256]{0,1:T(8,128)(2,1)}), bf16[1024,1024]{0,1:T(8,128)(2,1)}) %all-gather.8.cloned.1.call-update) | async-done | bytes 2097168 | tf_op jit(solution)/shard_map/all_gather | solution.py:52
  1039.2 16.0 %convolution_bitcast_fusion.1 = f32[4096,1024]{0,1:T(8,128)} fusion(bf16[1024,1024]{0,1:T(8,128)(2,1)} %all-gather.8.cloned.1.call-done, bf16[1024,4096]{1,0:T(8,128)(2,1)} %param.3), kind=kOutput, calls=%fused_computation.3 | convolution fusion | flops 8589934592 | bytes 27262976 | tf_op jit(solution)/shard_map/dot_general | solution.py:55
  1063.1 271.7 %reduce-scatter.8.cloned.1.call-done = f32[4096,128]{0,1:T(8,128)} async-done(((f32[4096,1024]{0,1:T(8,128)}), f32[4096,128]{0,1:T(8,128)}) %reduce-scatter.8.cloned.1.call-update) | async-done | bytes 2097168 | tf_op jit(solution)/shard_map/reduce_scatter | solution.py:54
  (129 shorter events, 172.0 us)
Async XLA Ops:
  7.2 130.7 %all-gather.4.cloned.1.call-start = ((), (), s32[]{:S(2)}) async-start(), calls=%async_computation.4 | async-start | bytes 9437184 | tf_op jit(solution)/shard_map/all_gather | solution.py:17
  10.0 185.6 %reduce-scatter.4.cloned.1.call-start = ((), (), s32[]{:S(2)}) async-start(), calls=%async_computation.5 | async-start | bytes 5242880 | tf_op jit(solution)/shard_map/reduce_scatter | solution.py:20
  152.9 188.0 %all-gather.6.cloned.1.call-start = ((), (), s32[]{:S(2)}) async-start(), calls=%async_computation.6 | async-start | bytes 5242880 | tf_op jit(solution)/shard_map/all_gather | solution.py:31
  308.2 207.4 %all-reduce.3.cloned.1.call-start = ((), (), s32[]{:S(2)}) async-start(), calls=%async_computation.7 | async-start | bytes 8388608 | tf_op jit(solution)/shard_map/psum | solution.py:35
  359.1 656.2 %reduce-scatter.6.cloned.1.call-start = ((), (), s32[]{:S(2)}) async-start(), calls=%async_computation.8 | async-start | bytes 9437184 | tf_op jit(solution)/shard_map/reduce_scatter | solution.py:44
  525.8 2.0 copy-start
  837.0 4.3 copy-start.1
  846.3 15.2 %slice-start = ((s8[16777216]{0:T(1024)(128)(4,1)}), s8[4194304]{0:T(1024)(128)(4,1)S(1)}, s32[]{:S(2)}) async-start(s8[16777216]{0:T(1024)(128)(4,1)} %bitcast.120), calls=%async_computation.11 | async-start | bytes 8388608
  849.5 12.0 slice-start.1
  850.0 11.6 slice-start.2
  853.6 7.9 slice-start.3
  868.3 171.0 %all-gather.8.cloned.1.call-start = ((), (), s32[]{:S(2)}) async-start(), calls=%async_computation.9 | async-start | bytes 2621440 | tf_op jit(solution)/shard_map/all_gather | solution.py:52
  1017.4 317.4 %reduce-scatter.8.cloned.1.call-start = ((), (), s32[]{:S(2)}) async-start(), calls=%async_computation.10 | async-start | bytes 18874368 | tf_op jit(solution)/shard_map/reduce_scatter | solution.py:54
Sparse Core Ops, SparseCore 0:
  10.7 127.1 all-gather.3
  153.0 42.5 reduce-scatter.3
  308.3 32.5 all-gather.5
  359.2 156.3 all-reduce.2
  868.4 146.8 reduce-scatter.5
  1017.5 21.6 all-gather.7
  1055.3 279.4 reduce-scatter.7
